TPU v7x, 32 devices: a whole 2x2x4 slice. The times are simulated.
32 devices in a mesh: freq: 2 (over x), param: 4 (over y, core), sens: 4 (over z).
Axes of the slice: x: 2, y: 2, z: 4, core: 2. Of those that a mesh axis runs over, the one named last changes fastest.
Arguments:
- series: bfloat16 [8, 600, 52], P(None, 'sens', 'freq'), may hold values from -6 to 6
- kernel: bfloat16 [2, 32, 600, 4096], P(None, 'freq', 'sens', 'param'), may hold values from -0.1875 to 0.1875
- prior_spectrum: float32 [32], P('freq'), may hold values from 0.3 to 1.5
- prior_scale: float32 [4096], P('param'), may hold values from 0.5 to 2
Outputs:
- adjoint_map: float32 [52, 8, 4096], P('freq', 'sens', 'param')
All inputs are finite; a program needn't handle non-finite values.
Results may differ from a plain program's by a relative error of at most 0.0047.
Values may be sent and summed in bfloat16 or wider, within the bound.
A program may use at most 64 MiB of HBM per device.

v0:
```python
import math

import jax
import jax.numpy as jnp
from jax import lax
from jax.sharding import PartitionSpec as P

LEN = 840
FB_DEV = 16


def extended(cells, sides, width):
    for axis, dim in sides:
        count = lax.axis_size(axis)
        ends = count - 1
        head = lax.slice_in_dim(cells, 0, width, axis=dim)
        tail = lax.slice_in_dim(cells, cells.shape[dim] - width, cells.shape[dim], axis=dim)
        cells = jnp.concatenate(
            [
                lax.ppermute(tail, axis, [(i, (i + 1) % count) for i in range(ends)]),
                cells,
                lax.ppermute(head, axis, [((i + 1) % count, i) for i in range(ends)]),
            ],
            axis=dim,
        )
    return cells


def phase_tables(bin_first, bin_count, time_count):
    bin_index = bin_first + jnp.arange(bin_count, dtype=jnp.int32)
    time_index = jnp.arange(time_count, dtype=jnp.int32)
    product = time_index[:, None] * bin_index[None, :] % LEN
    phase_angle = product.astype(jnp.float32) * (2.0 * math.pi / LEN)
    return (jnp.cos(phase_angle), jnp.sin(phase_angle))


def contract(spectrum, operator):
    return jnp.einsum("bsr,bsp->brp", spectrum, operator, preferred_element_type=jnp.float32)


def local(series, kernel, prior_spectrum, prior_scale):
    highest = lax.Precision.HIGHEST
    groups = lax.axis_size("freq")
    first_bin = lax.axis_index("freq") * FB_DEV
    probes, sens_dev, time_dev = series.shape
    total_times = time_dev * groups
    cosine, sine_part = phase_tables(first_bin, FB_DEV, total_times)
    phase_table = jnp.concatenate([cosine, -sine_part], axis=1)
    series_piece = lax.all_gather(series, "freq", axis=2, tiled=True)
    row_count = series_piece.shape[2]
    flat_rows = series_piece.astype(jnp.float32).reshape(-1, row_count)
    spectra = jnp.dot(flat_rows, phase_table, precision=highest)
    spectra = (spectra * (1.0 / math.sqrt(total_times))).astype(jnp.bfloat16)
    both_parts = (
        spectra.reshape(probes, sens_dev, 2, FB_DEV)
        .transpose(3, 1, 2, 0)
        .reshape(FB_DEV, sens_dev, 2 * probes)
    )
    with_real = contract(both_parts, kernel[0])
    with_imag = contract(both_parts, kernel[1])
    real_part = with_real[:, :probes] + with_imag[:, probes:]
    imag_part = with_real[:, probes:] - with_imag[:, :probes]
    partial_value = jnp.stack([real_part, imag_part])
    summed = lax.psum_scatter(partial_value, "sens", scatter_dimension=2, tiled=True)
    weights = prior_spectrum * (1.0 / math.sqrt(FB_DEV * groups))
    scaled_spec = summed * weights[None, :, None, None]
    arrived = lax.all_to_all(scaled_spec, "freq", split_axis=3, concat_axis=1, tiled=True)
    bin_total = arrived.shape[1]
    item_count = arrived.shape[2]
    col_count = arrived.shape[3]
    cos_all, sin_all = phase_tables(0, bin_total, total_times)
    full_table = jnp.concatenate([cos_all, -sin_all], axis=1)
    flat_rows = arrived.reshape(2 * bin_total, item_count * col_count)
    arranged = jnp.dot(full_table, flat_rows, precision=highest).reshape(
        total_times, item_count, col_count
    )
    image_field = lax.all_to_all(arranged, "freq", split_axis=0, concat_axis=2, tiled=True)
    weighted = image_field * prior_scale
    padded = extended(weighted, (("param", 2),), 1)
    smooth = 0.5 * weighted + 0.25 * (padded[:, :, :-2] + padded[:, :, 2:])
    return smooth * prior_scale


def solution(mesh):
    placed = (P(None, "sens", "freq"), P(None, "freq", "sens", "param"), P("freq"), P("param"))
    return jax.shard_map(
        local, mesh=mesh, in_specs=placed, out_specs=P("freq", "sens", "param"), check_vma=False
    )
```

profile of v0, /device:TPU:1, one launch (start us, length us, event | category | flops | bytes accessed | tf_op | source)
XLA Modules:
  0.0 111.2 jit_solution(6841817095177923095)
XLA Ops:
  6.5 0.0 reduce-scatter.2.cloned.1.call-start
  6.5 0.1 fusion.32
  6.7 5.6 %all_gather.3 = bf16[8,150,52]{1,0,2:T(8,128)(2,1)S(1)} all-gather(bf16[8,150,26]{1,0,2:T(8,128)(2,1)} %param.4), channel_id=1, replica_groups=mesh['freq'=2,'param'=4,'sens'=4] {'freq'}, dimensions={2}, use_global_device_ids=true | all-gather | bytes 187200 | tf_op jit(solution)/shard_map/all_gather | solution.py:49
  12.3 0.2 reshape.21
  12.5 0.2 fusion.3
  12.8 0.2 reshape.22
  13.0 7.8 %fusion.36 = (bf16[1,16,150,1024]{3,1,2,0:T(8,128)(2,1)S(1)}, bf16[1,16,150,1024]{3,1,2,0:T(8,128)(2,1)}) fusion(bf16[2,16,150,1024]{3,1,2,0:T(8,128)(2,1)} %param.5), kind=kLoop, calls=%fused_computation.55 | loop fusion | bytes 19660800 | tf_op jit(solution)/shard_map/slice | solution.py:59
  20.8 7.8 %fusion = f32[16,16,1024]{2,1,0:T(8,128)S(1)} fusion(bf16[1,16,150,1024]{3,1,2,0:T(8,128)(2,1)} %get-tuple-element.6, bf16[8,150,2,16]{1,0,3,2:T(8,128)(2,1)S(1)} %reshape.22), kind=kOutput, calls=%fused_computation.1 | convolution fusion | flops 78643200 | bytes 6040576 | tf_op jit(solution)/shard_map/bsr,bsp->brp/dot_general | solution.py:38
  28.6 5.6 %fusion.1 = f32[16,16,1024]{2,1,0:T(8,128)S(1)} fusion(bf16[1,16,150,1024]{3,1,2,0:T(8,128)(2,1)S(1)} %get-tuple-element.5, bf16[8,150,2,16]{1,0,3,2:T(8,128)(2,1)S(1)} %reshape.22), kind=kOutput, calls=%fused_computation.3 | convolution fusion | flops 78643200 | bytes 6040576 | tf_op jit(solution)/shard_map/bsr,bsp->brp/dot_general | solution.py:38
  34.2 0.0 copy-start.1
  34.2 0.1 fusion.5
  34.3 0.1 pad_maximum_fusion
  34.4 1.6 %copy.43 = f32[2,16,8,1024]{3,1,0,2:T(8,128)} copy(f32[2,16,8,1024]{3,2,1,0:T(8,128)S(1)} %pad_maximum_fusion) | data formatting | bytes 2097152 | tf_op jit(solution)/shard_map/stack | solution.py:63
  36.0 0.0 reduce-scatter.2.cloned.1.call-update
  36.0 0.0 copy-done.1
  36.0 29.0 %reduce-scatter.2.cloned.1.call-done = f32[2,16,2,1024]{3,1,0,2:T(8,128)} async-done(((f32[2,16,8,1024]{3,1,0,2:T(8,128)}), f32[2,16,2,1024]{3,1,0,2:T(8,128)}) %reduce-scatter.2.cloned.1.call-update) | async-done | bytes 262160 | tf_op jit(solution)/shard_map/reduce_scatter | solution.py:64
  65.1 1.0 broadcast_multiply_fusion
  66.1 1.3 %copy.44 = f32[2,16,2,1024]{1,2,0,3:T(2,128)S(1)} copy(f32[2,16,2,1024]{3,1,0,2:T(8,128)S(1)} %broadcast_multiply_fusion) | data formatting | bytes 524288 | tf_op jit(solution)/shard_map/mul | solution.py:66
  67.5 0.0 copy-start
  67.5 3.6 %reshape.26 = f32[2,1,32768]{2,1,0:T(1,128)} reshape(f32[1024,2,2,16]{3,2,1,0:T(2,128)S(1)} %bitcast.53) | data formatting | bytes 524288
  71.0 3.4 %all-to-all-start = ((f32[2,1,32768]{2,1,0:T(1,128)}), f32[2,1,32768]{2,1,0:T(1,128)S(1)}, u32[]{:S(2)}, u32[]{:S(2)}) async-start(f32[2,1,32768]{2,1,0:T(1,128)} %reshape.26), calls=%async_computation.1 | async-start | bytes 524288 | tf_op jit(solution)/shard_map/all_to_all | solution.py:67
  74.5 0.1 sine_negate_fusion
  74.6 3.9 %all-to-all-done = f32[2,1,32768]{2,1,0:T(1,128)S(1)} async-done(((f32[2,1,32768]{2,1,0:T(1,128)}), f32[2,1,32768]{2,1,0:T(1,128)S(1)}, u32[]{:S(2)}, u32[]{:S(2)}) %all-to-all-start) | async-done | bytes 262176 | tf_op jit(solution)/shard_map/all_to_all | solution.py:67
  78.5 0.5 broadcast.17
  79.0 1.4 %reduce = f32[2,32768]{1,0:T(2,128)S(1)} reduce(f32[2,1,32768]{2,1,0:T(1,128)S(1)} %all-to-all-done, f32[]{:T(128)} %broadcast.17), dimensions={1}, to_apply=%all_to_all.24.reduce_sub_computation | reduce | bytes 524292 | tf_op jit(solution)/shard_map/all_to_all | solution.py:67
  80.5 2.8 %reshape.27 = f32[1024,2,2,16]{3,2,1,0:T(2,128)S(1)} reshape(f32[2,32768]{1,0:T(2,128)S(1)} %reduce) | data formatting | bytes 524288
  83.3 1.5 %copy.45 = f32[2,16,2,2,512]{4,2,1,3,0:T(2,128)S(1)} copy(f32[2,16,2,2,512]{1,2,0,4,3:T(2,128)S(1)} %bitcast.54) | data formatting | bytes 524288 | tf_op jit(solution)/shard_map/all_to_all | solution.py:67
  84.7 0.4 fusion.6
  85.1 0.2 copy.47
  85.3 6.1 %all_to_all.33 = f32[52,2,512]{2,1,0:T(2,128)S(1)} all-to-all(f32[52,2,512]{2,1,0:T(2,128)S(1)} %copy.47), channel_id=1, replica_groups=mesh['freq'=2,'param'=4,'sens'=4] {'freq'}, dimensions={0} | all-to-all | bytes 425984 | tf_op jit(solution)/shard_map/all_to_all | solution.py:77
  91.4 0.0 copy-done
  91.5 0.1 broadcast_multiply_fusion.1
  91.5 0.1 fusion.37
  91.6 6.4 %collective-permute-start = (f32[26,2,1]{2,1,0:T(2,128)S(1)}, f32[26,2,1]{2,1,0:T(2,128)S(1)}, u32[]{:S(2)}, u32[]{:S(2)}) collective-permute-start(f32[26,2,1]{2,1,0:T(2,128)S(1)} %get-tuple-element.9), channel_id=1, source_target_pairs={{0,4},{4,8},{8,12},{1,5},{5,9},{9,13},{2,6},{6,10},{10,14},{3,7},{... | collective-permute-start | bytes 632 | tf_op jit(solution)/shard_map/ppermute | solution.py:20
  98.0 1.9 %collective-permute-start.1 = (f32[26,2,1]{2,1,0:T(2,128)S(1)}, f32[26,2,1]{2,1,0:T(2,128)S(1)}, u32[]{:S(2)}, u32[]{:S(2)}) collective-permute-start(f32[26,2,1]{2,1,0:T(2,128)S(1)} %get-tuple-element.10), channel_id=1, source_target_pairs={{4,0},{8,4},{12,8},{5,1},{9,5},{13,9},{6,2},{10,6},{14,10},{7,3},{... | collective-permute-start | bytes 632 | tf_op jit(solution)/shard_map/ppermute | solution.py:22
  99.9 0.0 collective-permute-done
  99.9 3.2 %collective-permute-done.1 = f32[26,2,1]{2,1,0:T(2,128)S(1)} collective-permute-done((f32[26,2,1]{2,1,0:T(2,128)S(1)}, f32[26,2,1]{2,1,0:T(2,128)S(1)}, u32[]{:S(2)}, u32[]{:S(2)}) %collective-permute-start.1) | collective-permute-done | bytes 240 | tf_op jit(solution)/shard_map/ppermute | solution.py:22
  103.2 1.2 %fusion.12 = f32[26,2,1024]{2,1,0:T(2,128)} fusion(f32[26,2,1]{2,1,0:T(2,128)S(1)} %collective-permute-done.1, f32[26,2,1024]{2,1,0:T(2,128)S(1)} %broadcast_multiply_fusion.1, f32[26,2,1]{2,1,0:T(2,128)S(1)} %collective-permute-done, f32[1024]{0:T(1024)S(1)} %copy-done), kind=kLoop, calls=%fused_computation.20 | loop fusion | flops 372736 | bytes 430496 | tf_op jit(solution)/shard_map/mul | solution.py:81
  (3 shorter events, 0.0 us)
Async XLA Ops:
  6.5 58.5 %reduce-scatter.2.cloned.1.call-start = ((), (), s32[]{:S(2)}) async-start(), calls=%async_computation.3 | async-start | bytes 1310720 | tf_op jit(solution)/shard_map/reduce_scatter | solution.py:64
  34.2 1.8 %copy-start.1 = (f32[16]{0:T(128)S(1)}, f32[16]{0:T(128)}, u32[]{:S(2)}) copy-start(f32[16]{0:T(128)} %param.6) | copy-start | bytes 196
  67.5 24.0 %copy-start = (f32[1024]{0:T(1024)S(1)}, f32[1024]{0:T(1024)}, u32[]{:S(2)}) copy-start(f32[1024]{0:T(1024)} %param.7) | copy-start | bytes 12292
  71.0 7.5 %all-to-all-start = ((f32[2,1,32768]{2,1,0:T(1,128)}), f32[2,1,32768]{2,1,0:T(1,128)S(1)}, u32[]{:S(2)}, u32[]{:S(2)}) async-start(f32[2,1,32768]{2,1,0:T(1,128)} %reshape.26), calls=%async_computation.1 | async-start | bytes 524288 | tf_op jit(solution)/shard_map/all_to_all | solution.py:67
  91.6 8.3 %collective-permute-start = (f32[26,2,1]{2,1,0:T(2,128)S(1)}, f32[26,2,1]{2,1,0:T(2,128)S(1)}, u32[]{:S(2)}, u32[]{:S(2)}) collective-permute-start(f32[26,2,1]{2,1,0:T(2,128)S(1)} %get-tuple-element.9), channel_id=1, source_target_pairs={{0,4},{4,8},{8,12},{1,5},{5,9},{9,13},{2,6},{6,10},{10,14},{3,7},{... | collective-permute-start | bytes 632 | tf_op jit(solution)/shard_map/ppermute | solution.py:20
  98.0 5.2 %collective-permute-start.1 = (f32[26,2,1]{2,1,0:T(2,128)S(1)}, f32[26,2,1]{2,1,0:T(2,128)S(1)}, u32[]{:S(2)}, u32[]{:S(2)}) collective-permute-start(f32[26,2,1]{2,1,0:T(2,128)S(1)} %get-tuple-element.10), channel_id=1, source_target_pairs={{4,0},{8,4},{12,8},{5,1},{9,5},{13,9},{6,2},{10,6},{14,10},{7,3},{... | collective-permute-start | bytes 632 | tf_op jit(solution)/shard_map/ppermute | solution.py:22
Sparse Core Ops, SparseCore 0:
  36.1 28.8 reduce-scatter.1
where the time goes:
time: 112 us; the launch traced here: 111 us
  waiting for transfers between devices  36.2 us (32%)
  local copies, waits for them, and re-layouts  19.8 us (18%)
  matrix products  14 us (12%)
  between operations  13.6 us (12%)
  starting transfers between devices  11.7 us (10%)
  blocking collectives  11.7 us (10%)
  other arithmetic  4.27 us (4%)
    reduce_scatter x1, waiting for transfers between devices, local(): lax.psum_scatter(partial_value, 'sens', scatter_dimension=2, tiled=True)  29 us
    dot_general x2, matrix products, contract(): jnp.einsum('bsr,bsp->brp', spectrum, operator, preferred_element_type=jnp...  13.4 us
    slice x1, local copies, waits for them, and re-layouts, local(): with_real = contract(both_parts, kernel[0])  7.77 us
    unnamed x6, local copies, waits for them, and re-layouts  6.39 us
    ppermute x1, starting transfers between devices, extended(): lax.ppermute(tail, axis, [(i, (i + 1) % count) for i in range(ends)])  6.36 us
    all_to_all x1, blocking collectives, local(): lax.all_to_all(arranged, 'freq', split_axis=0, concat_axis=2, tiled=True)  6.12 us
    all_gather x1, blocking collectives, local(): series_piece = lax.all_gather(series, 'freq', axis=2, tiled=True)  5.63 us
    all_to_all x1, waiting for transfers between devices, local(): lax.all_to_all(scaled_spec, 'freq', split_axis=3, concat_axis=1, tiled=True)  3.86 us
  transfers between devices with their start and end apart: 4, of which 3 were waited for; matrix products, arithmetic and copies ran while one was open for 0% of the time, Pallas kernels for 0%

commit v1 on v0

v1 whole, which is shorter than its diff:
```python
import functools
import math

import jax
import jax.numpy as jnp
import numpy as np
from jax import lax
from jax.experimental import pallas as pl
from jax.experimental.pallas import tpu as pltpu
from jax.sharding import PartitionSpec as P

LEN = 840
MESH = pl.DeviceIdType.MESH
BF16 = jnp.bfloat16
F32 = jnp.float32


def split(table):
    high = table.astype(BF16)
    low = (table - high.astype(np.float32)).astype(BF16)
    return high, low


def trig(bins, times):
    angle = 2.0 * np.pi * ((np.arange(times)[:, None] * np.arange(bins)[None, :]) % LEN) / LEN
    return np.cos(angle), np.sin(angle)


def spectrum_tables(groups, bins_dev, time_dev, probes):
    cosine, sine = trig(groups * bins_dev, groups * time_dev)
    scale = 1.0 / math.sqrt(groups * time_dev)
    both = np.stack([cosine, -sine], axis=0) * scale
    both = both.reshape(2, groups * time_dev, groups, bins_dev).transpose(2, 0, 3, 1)
    flat = np.repeat(both.reshape(groups, 2 * bins_dev, -1), probes, axis=-1).astype(np.float32)
    high, low = split(flat)
    return np.stack([high, low], axis=1)


def pick_tables(bins_dev, senses, keep):
    split_by = (bins_dev // 8, senses, 8, 2, keep)
    half, _, inner, part, _ = np.indices(split_by).reshape(len(split_by), -1)
    rows = np.arange(half.size)
    bins = half * 8 + inner
    first = np.zeros((half.size, 2 * bins_dev), np.float32)
    second = np.zeros_like(first)
    first[rows, part * bins_dev + bins] = 1.0
    second[rows, (1 - part) * bins_dev + bins] = np.where(part == 0, 1.0, -1.0)
    return np.stack([first, second]).astype(BF16)


def image_tables(groups, bins_dev, time_dev, keep):
    cosine, sine = trig(groups * bins_dev, groups * time_dev)
    both = np.stack([cosine, -sine], axis=2).reshape(groups, time_dev, groups, bins_dev, 2)
    both = both.transpose(2, 0, 1, 3, 4)
    full = np.einsum("ghtbc,qr->ghtqbcr", both, np.eye(keep)).astype(np.float32)
    flat = full.reshape(groups, groups, time_dev * keep, bins_dev * 2 * keep)
    high, low = split(flat)
    return np.concatenate([high, low, high], axis=-1)


def body(
    cfg,
    series_hbm,
    kernel_hbm,
    prior_hbm,
    scale_hbm,
    spec_hbm,
    img_hbm,
    pick_hbm,
    out_ref,
    kbuf,
    prior,
    scale,
    spec_tab,
    img_tab,
    pick,
    gathered,
    wide,
    spread,
    left_mat,
    weight,
    sbuf,
    rbuf,
    own,
    xsend,
    xrecv,
    halo_left,
    halo_right,
    small_sem,
    k_sem,
    g_send,
    g_recv,
    z_send,
    z_recv,
    x_send,
    x_recv,
    hl_send,
    hl_recv,
    hr_send,
    hr_recv,
):
    groups, params, senses, chunks = cfg
    f = lax.axis_index("freq")
    k = lax.axis_index("param")
    s = lax.axis_index("sens")
    _, sens_dev, bins_dev, _ = kernel_hbm.shape
    halves = bins_dev // 8
    width = kbuf.shape[-1]
    block = wide.shape[2] // halves
    probes = block // 16
    keep = probes // senses
    edge = halo_left.shape[-1]

    def freq_peer(d):
        return lax.rem(f + d, groups)

    def sens_peer(d):
        return lax.rem(s + d, senses)

    small = [
        pltpu.make_async_copy(series_hbm, gathered.at[f], small_sem.at[0]),
        pltpu.make_async_copy(spec_hbm.at[f], spec_tab, small_sem.at[1]),
        pltpu.make_async_copy(prior_hbm, prior, small_sem.at[2]),
        pltpu.make_async_copy(scale_hbm, scale, small_sem.at[3]),
        pltpu.make_async_copy(img_hbm.at[f], img_tab, small_sem.at[4]),
        pltpu.make_async_copy(pick_hbm, pick, small_sem.at[5]),
    ]
    for copy in small:
        copy.start()
    loads = [
        [
            pltpu.make_async_copy(
                kernel_hbm.at[part, :, pl.ds(h * 8, 8), pl.ds(c * width, width)],
                kbuf.at[c, part, h],
                k_sem.at[c, part, h],
            )
            for h in range(halves)
            for part in range(2)
        ]
        for c in range(chunks)
    ]
    for group in loads:
        for copy in group:
            copy.start()

    barrier = pltpu.get_barrier_semaphore()
    for d in range(1, groups):
        pl.semaphore_signal(
            barrier, inc=1, device_id={"freq": freq_peer(d)}, device_id_type=MESH
        )
    for d in range(1, senses):
        pl.semaphore_signal(
            barrier, inc=1, device_id={"sens": sens_peer(d)}, device_id_type=MESH
        )
    has_left = k > 0
    has_right = k < params - 1

    @pl.when(has_left)
    def _():
        for d in range(groups):
            pl.semaphore_signal(
                barrier,
                inc=1,
                device_id={"freq": freq_peer(d), "param": k - 1},
                device_id_type=MESH,
            )

    @pl.when(has_right)
    def _():
        for d in range(groups):
            pl.semaphore_signal(
                barrier,
                inc=1,
                device_id={"freq": freq_peer(d), "param": k + 1},
                device_id_type=MESH,
            )

    small[0].wait()
    peers = groups + senses - 2
    beside = jnp.where(has_left, groups, 0) + jnp.where(has_right, groups, 0)
    pl.semaphore_wait(barrier, peers + beside)

    def series_copy(slot, target):
        return pltpu.make_async_remote_copy(
            src_ref=gathered.at[f],
            dst_ref=gathered.at[slot],
            send_sem=g_send.at[target],
            recv_sem=g_recv.at[slot],
            device_id={"freq": target},
            device_id_type=MESH,
        )

    for d in range(1, groups):
        series_copy(f, freq_peer(d)).start()
    for copy in small[1:]:
        copy.wait()
    probe_row = wide.shape[2]
    row = lax.broadcasted_iota(jnp.int32, (probe_row, wide.shape[3]), 0)
    lane = lax.broadcasted_iota(jnp.int32, (probe_row, wide.shape[3]), 1)
    probe = (row // (16 * keep)) % senses * keep + row % keep
    same = lane % probes == probe
    for v in range(2):
        for i in range(2):
            full = jnp.dot(pick[v], spec_tab[i], preferred_element_type=F32)
            wide[v, i] = jnp.where(same, full, 0.0).astype(BF16)
    row = lax.broadcasted_iota(jnp.int32, spread.shape, 0)
    lane = lax.broadcasted_iota(jnp.int32, spread.shape, 1)
    spread[...] = jnp.where(lane // 8 == row, 1.0, 0.0).astype(BF16)
    norm = 1.0 / math.sqrt(bins_dev * groups)
    row = lax.broadcasted_iota(jnp.int32, weight.shape[1:], 0)
    for h in range(halves):
        value = jnp.zeros(weight.shape[1:], F32)
        for b in range(8):
            value = jnp.where(row // (2 * keep) == b, prior[h * 8 + b] * norm, value)
        weight[h] = value

    for d in range(1, groups):
        series_copy(freq_peer(d), freq_peer(d)).wait_recv()
    rows = jnp.concatenate([gathered[g] for g in range(groups)], axis=0)
    row = lax.broadcasted_iota(jnp.int32, (block, spread.shape[1]), 0)
    lane = lax.broadcasted_iota(jnp.int32, (block, spread.shape[1]), 1)
    same = lane % 8 == row // (2 * keep) % 8
    for h in range(halves):
        for v in range(2):
            spec = jnp.dot(
                wide[v, 0, h * block : (h + 1) * block], rows, preferred_element_type=F32
            ) + jnp.dot(
                wide[v, 1, h * block : (h + 1) * block], rows, preferred_element_type=F32
            )
            full = jnp.dot(spec.astype(BF16), spread[...], preferred_element_type=F32)
            left_mat[v, h] = jnp.where(same, full, 0.0).astype(BF16)


    def z_copy(target, slot, c):
        return pltpu.make_async_remote_copy(
            src_ref=sbuf.at[target, c],
            dst_ref=rbuf.at[slot, c],
            send_sem=z_send.at[target, c],
            recv_sem=z_recv.at[slot, c],
            device_id={"sens": target},
            device_id_type=MESH,
        )

    for c in range(chunks):
        for h in range(halves):
            total = jnp.zeros((block, width), F32)
            for part in range(2):
                loads[c][h * 2 + part].wait()
                right_mat = kbuf.at[c, part, h].reshape(sens_dev * 8, width)[...]
                total = total + jnp.dot(
                    left_mat[part, h], right_mat, preferred_element_type=F32
                )
            each = block // senses
            for j in range(senses):
                piece = total[j * each : (j + 1) * each] * weight[h]
                sbuf[j, c, h * each : (h + 1) * each, :] = piece.astype(BF16)
        for d in (2, 1, 3) if senses == 4 else range(1, senses):
            z_copy(sens_peer(d), s, c).start()

    def x_copy(target, slot, c):
        return pltpu.make_async_remote_copy(
            src_ref=xsend.at[target, c],
            dst_ref=xrecv.at[slot, c],
            send_sem=x_send.at[target, c],
            recv_sem=x_recv.at[slot, c],
            device_id={"freq": target},
            device_id_type=MESH,
        )

    def to_left(target, slot):
        return pltpu.make_async_remote_copy(
            src_ref=xsend.at[target, 0, :, pl.ds(0, edge)],
            dst_ref=halo_right.at[slot],
            send_sem=hl_send.at[target],
            recv_sem=hr_recv.at[slot],
            device_id={"freq": target, "param": jnp.maximum(k - 1, 0)},
            device_id_type=MESH,
        )

    def to_right(target, slot):
        return pltpu.make_async_remote_copy(
            src_ref=xsend.at[target, chunks - 1, :, pl.ds(width - edge, edge)],
            dst_ref=halo_left.at[slot],
            send_sem=hr_send.at[target],
            recv_sem=hl_recv.at[slot],
            device_id={"freq": target, "param": jnp.minimum(k + 1, params - 1)},
            device_id_type=MESH,
        )

    for c in range(chunks):
        total = sbuf[s, c].astype(F32)
        for d in range(1, senses):
            z_copy(sens_peer(d), sens_peer(d), c).wait_recv()
            total = total + rbuf[sens_peer(d), c].astype(F32)
        high = total.astype(BF16)
        low = (total - high.astype(F32)).astype(BF16)
        stacked = jnp.concatenate([high, high, low], axis=0)
        lanes = scale[:, c * width : (c + 1) * width]
        for d in list(range(1, groups)) + [0]:
            g = freq_peer(d)
            image = jnp.dot(img_tab[g], stacked, preferred_element_type=F32) * lanes
            if d == 0:
                own[c] = image
                if c == 0 or c == chunks - 1:
                    xsend[g, c] = image.astype(BF16)
            else:
                xsend[g, c] = image.astype(BF16)
                x_copy(g, f, c).start()
        if c == 0:

            @pl.when(has_left)
            def _():
                for d in range(groups):
                    to_left(freq_peer(d), f).start()

        if c == chunks - 1:

            @pl.when(has_right)
            def _():
                for d in range(groups):
                    to_right(freq_peer(d), f).start()

    for c in range(chunks):
        image = own[c]
        for d in range(1, groups):
            g = freq_peer(d)
            x_copy(g, g, c).wait_recv()
            image = image + xrecv[g, c].astype(F32)
        own[c] = image


    @pl.when(has_left)
    def _():
        for d in range(groups):
            to_right(freq_peer(d), freq_peer(d)).wait_recv()

    @pl.when(jnp.logical_not(has_left))
    def _():
        halo_left[...] = jnp.zeros_like(halo_left)

    @pl.when(has_right)
    def _():
        for d in range(groups):
            to_left(freq_peer(d), freq_peer(d)).wait_recv()

    @pl.when(jnp.logical_not(has_right))
    def _():
        halo_right[...] = jnp.zeros_like(halo_right)

    left = halo_left[0].astype(F32)
    right = halo_right[0].astype(F32)
    for g in range(1, groups):
        left = left + halo_left[g].astype(F32)
        right = right + halo_right[g].astype(F32)
    for c in range(chunks):
        mid = own[c]
        before = own[c - 1][:, width - 1 :] if c > 0 else left[:, edge - 1 :]
        after = own[c + 1][:, :1] if c < chunks - 1 else right[:, :1]
        lower = jnp.concatenate([before, mid[:, :-1]], axis=1)
        upper = jnp.concatenate([mid[:, 1:], after], axis=1)
        lanes = scale[:, c * width : (c + 1) * width]
        out_ref[:, c * width : (c + 1) * width] = lanes * (0.5 * mid + 0.25 * (lower + upper))

    for d in range(1, groups):
        series_copy(f, freq_peer(d)).wait_send()
        for c in range(chunks):
            x_copy(freq_peer(d), f, c).wait_send()
    for c in range(chunks):
        for d in range(1, senses):
            z_copy(sens_peer(d), s, c).wait_send()

    @pl.when(has_left)
    def _():
        for d in range(groups):
            to_left(freq_peer(d), f).wait_send()

    @pl.when(has_right)
    def _():
        for d in range(groups):
            to_right(freq_peer(d), f).wait_send()


def local(mesh_shape, series, kernel, prior_spectrum, prior_scale):
    groups, params, senses = (mesh_shape[n] for n in ("freq", "param", "sens"))
    probes, sens_dev, time_dev = series.shape
    _, bins_dev, _, cols = kernel.shape
    keep = probes // senses
    chunks = 4
    width = cols // chunks
    edge = min(128, width)
    rows = time_dev * keep
    depth = bins_dev * 2 * keep
    halves = bins_dev // 8
    block = 16 * probes
    spec_tab = spectrum_tables(groups, bins_dev, time_dev, probes)
    pick_tab = pick_tables(bins_dev, senses, keep)
    img_tab = image_tables(groups, bins_dev, time_dev, keep)
    dma = pltpu.SemaphoreType.DMA
    out = pl.pallas_call(
        functools.partial(body, (groups, params, senses, chunks)),
        out_shape=jax.ShapeDtypeStruct((rows, cols), F32),
        in_specs=[pl.BlockSpec(memory_space=pltpu.HBM)] * 7,
        out_specs=pl.BlockSpec(memory_space=pltpu.VMEM),
        scratch_shapes=[
            pltpu.VMEM((chunks, 2, halves, sens_dev, 8, width), BF16),
            pltpu.SMEM((bins_dev,), F32),
            pltpu.VMEM((1, cols), F32),
            pltpu.VMEM(spec_tab.shape[1:], BF16),
            pltpu.VMEM(img_tab.shape[1:], BF16),
            pltpu.VMEM(pick_tab.shape, BF16),
            pltpu.VMEM((groups, time_dev * probes, sens_dev), BF16),
            pltpu.VMEM((2, 2, halves * block, groups * time_dev * probes), BF16),
            pltpu.VMEM((sens_dev, sens_dev * 8), BF16),
            pltpu.VMEM((2, halves, block, sens_dev * 8), BF16),
            pltpu.VMEM((halves, block // senses, width), F32),
            pltpu.VMEM((senses, chunks, depth, width), BF16),
            pltpu.VMEM((senses, chunks, depth, width), BF16),
            pltpu.VMEM((chunks, rows, width), F32),
            pltpu.VMEM((groups, chunks, rows, width), BF16),
            pltpu.VMEM((groups, chunks, rows, width), BF16),
            pltpu.VMEM((groups, rows, edge), BF16),
            pltpu.VMEM((groups, rows, edge), BF16),
            dma((6,)),
            dma((chunks, 2, halves)),
            dma((groups,)),
            dma((groups,)),
            dma((senses, chunks)),
            dma((senses, chunks)),
            dma((groups, chunks)),
            dma((groups, chunks)),
            dma((groups,)),
            dma((groups,)),
            dma((groups,)),
            dma((groups,)),
        ],
        compiler_params=pltpu.CompilerParams(
            collective_id=0, has_side_effects=True, vmem_limit_bytes=60 * 1024 * 1024
        ),
    )(
        series.transpose(2, 0, 1).reshape(time_dev * probes, sens_dev),
        kernel.transpose(0, 2, 1, 3),
        prior_spectrum,
        prior_scale.reshape(1, cols),
        jnp.asarray(spec_tab),
        jnp.asarray(img_tab),
        jnp.asarray(pick_tab),
    )
    return out.reshape(time_dev, keep, cols)


def solution(mesh):
    placed = (P(None, "sens", "freq"), P(None, "freq", "sens", "param"), P("freq"), P("param"))
    return jax.shard_map(
        functools.partial(local, dict(mesh.shape)),
        mesh=mesh,
        in_specs=placed,
        out_specs=P("freq", "sens", "param"),
        check_vma=False,
    )
```

time: 112 us -> 31.7 us (0.28)
  waiting for transfers between devices: 36.2 us -> 0 us
  Pallas kernels: 0 us -> 29.4 us
  local copies, waits for them, and re-layouts: 19.8 us -> 1.74 us
  matrix products: 14 us -> 0 us
  between operations: 13.6 us -> 0.01 us
  blocking collectives: 11.7 us -> 0 us
  starting transfers between devices: 11.7 us -> 0 us
  other arithmetic: 4.27 us -> 0 us
    pallas_call x0 -> x1, Pallas kernels: none -> 29.4 us  [local(): pl.pallas_call(functools.partial(body, (groups, params, senses, chunks)),...]
    reduce_scatter x1 -> x0, waiting for transfers between devices: 29 us -> none  [local(): lax.psum_scatter(partial_value, 'sens', scatter_dimension=2, tiled=True)]
    dot_general x4 -> x0, matrix products: 14 us -> none  [the longest x2 13.4 us: contract(): jnp.einsum('bsr,bsp->brp', spectrum, operator, preferred_element_type=jnp...]
    ppermute x2 -> x0, starting transfers between devices: 8.28 us -> none  [the longest x1 6.36 us: extended(): lax.ppermute(tail, axis, [(i, (i + 1) % count) for i in range(ends)])]
    slice x2 -> x0, local copies, waits for them, and re-layouts: 7.86 us -> none  [the longest x1 7.77 us: local(): with_real = contract(both_parts, kernel[0])]
    unnamed x6 -> x0, local copies, waits for them, and re-layouts: 6.39 us -> none
    all_to_all x1 -> x0, blocking collectives: 6.12 us -> none  [local(): lax.all_to_all(arranged, 'freq', split_axis=0, concat_axis=2, tiled=True)]
    all_gather x1 -> x0, blocking collectives: 5.63 us -> none  [local(): series_piece = lax.all_gather(series, 'freq', axis=2, tiled=True)]
  transfers between devices with their start and end apart: 4 -> 0, of which waited for: 3 -> 0; matrix products, arithmetic and copies ran while one was open for 0% -> 0% of each run, Pallas kernels for 0% -> 0%
where the time goes in v1:
time: 31.7 us; the launch traced here: 31.2 us
  Pallas kernels  29.4 us (93%)
  local copies, waits for them, and re-layouts  1.74 us (5%)
    pallas_call x1, Pallas kernels, local(): pl.pallas_call(functools.partial(body, (groups, params, senses, chunks)),...  29.4 us
    reshape x1, local copies, waits for them, and re-layouts, local(): return out.reshape(time_dev, keep, cols)  1.74 us

profile of v1, /device:TPU:1, one launch (start us, length us, event | category | flops | bytes accessed | tf_op | source)
XLA Modules:
  0.0 31.2 jit_solution(3839360082387945015)
XLA Ops:
  0.0 29.4 %shard_map.73 = f32[52,1024]{1,0:T(8,128)} custom-call(bf16[208,150]{1,0:T(8,128)(2,1)} %bitcast.6, bf16[2,150,16,1024]{3,2,1,0:T(8,128)(2,1)} %bitcast.5, f32[16]{0:T(128)} %prior_hbm.1, f32[1,1024]{1,0:T(1,128)} %bitcast.7, bf16[2,2,32,416]{3,2,1,0:T(8,128)(2,1)} %constant.6.clone.spec_hbm, bf16[2,2,52,192]{3,2,1,0:T(8,128)(2,1)} %constant.7.clone.img_hbm, ...), custom_call_target="tpu_custom_call" | custom-call | tf_op jit(solution)/shard_map/pallas_call | solution.py:399
  29.4 1.7 %reshape.11 = f32[26,2,1024]{2,1,0:T(2,128)} reshape(f32[52,1024]{1,0:T(8,128)} %shard_map.73) | data formatting | bytes 425984 | tf_op jit(solution)/shard_map/reshape | solution.py:448

commit v2 on v1

--- a/solution.py
+++ b/solution.py
@@ -81,6 +81,8 @@
     weight,
     sbuf,
     rbuf,
+    relay,
+    joined,
     own,
     xsend,
     xrecv,
@@ -92,6 +94,8 @@
     g_recv,
     z_send,
     z_recv,
+    relay_send,
+    relay_recv,
     x_send,
     x_recv,
     hl_send,
@@ -241,6 +245,102 @@
             device_id_type=MESH,
         )
 
+    paired = senses == 4
+    if paired:
+        pair = s + 1 - 2 * lax.rem(s, 2)
+        across = senses - 1 - s
+        other = senses - 1 - pair
+        outer = jnp.logical_or(s == 0, s == senses - 1)
+        inner = jnp.logical_not(outer)
+
+        @pl.when(inner)
+        def _():
+            rbuf[other] = jnp.zeros(rbuf.shape[1:], BF16)
+
+    def relay_copy(c):
+        return pltpu.make_async_remote_copy(
+            src_ref=sbuf.at[other, c],
+            dst_ref=relay.at[c],
+            send_sem=relay_send.at[c],
+            recv_sem=relay_recv.at[c],
+            device_id={"sens": pair},
+            device_id_type=MESH,
+        )
+
+    def joined_copy(c):
+        return pltpu.make_async_remote_copy(
+            src_ref=joined.at[c],
+            dst_ref=rbuf.at[s, c],
+            send_sem=z_send.at[across, c],
+            recv_sem=z_recv.at[s, c],
+            device_id={"sens": across},
+            device_id_type=MESH,
+        )
+
+    def send_sums(c):
+        if not paired:
+            for d in range(1, senses):
+                z_copy(sens_peer(d), s, c).start()
+            return
+
+        @pl.when(outer)
+        def _():
+            relay_copy(c).start()
+            z_copy(across, s, c).start()
+            z_copy(pair, s, c).start()
+
+        @pl.when(inner)
+        def _():
+            z_copy(other, s, c).start()
+            z_copy(pair, s, c).start()
+
+    def pass_on(c):
+        if not paired or c >= chunks:
+            return
+
+        @pl.when(inner)
+        def _():
+            relay_copy(c).wait_recv()
+            both = sbuf[across, c].astype(F32) + relay[c].astype(F32)
+            joined[c] = both.astype(BF16)
+            joined_copy(c).start()
+
+    def collect(c):
+        total = sbuf[s, c].astype(F32)
+        if not paired:
+            for d in range(1, senses):
+                z_copy(sens_peer(d), sens_peer(d), c).wait_recv()
+                total = total + rbuf[sens_peer(d), c].astype(F32)
+            return total
+        z_copy(pair, pair, c).wait_recv()
+
+        @pl.when(outer)
+        def _():
+            z_copy(other, other, c).wait_recv()
+
+        z_copy(across, across, c).wait_recv()
+        for slot in (pair, other, across):
+            total = total + rbuf[slot, c].astype(F32)
+        return total
+
+    def drain(c):
+        if not paired:
+            for d in range(1, senses):
+                z_copy(sens_peer(d), s, c).wait_send()
+            return
+
+        @pl.when(outer)
+        def _():
+            relay_copy(c).wait_send()
+            z_copy(across, s, c).wait_send()
+            z_copy(pair, s, c).wait_send()
+
+        @pl.when(inner)
+        def _():
+            z_copy(other, s, c).wait_send()
+            z_copy(pair, s, c).wait_send()
+            joined_copy(c).wait_send()
+
     for c in range(chunks):
         for h in range(halves):
             total = jnp.zeros((block, width), F32)
@@ -254,8 +354,7 @@
             for j in range(senses):
                 piece = total[j * each : (j + 1) * each] * weight[h]
                 sbuf[j, c, h * each : (h + 1) * each, :] = piece.astype(BF16)
-        for d in (2, 1, 3) if senses == 4 else range(1, senses):
-            z_copy(sens_peer(d), s, c).start()
+        send_sums(c)
 
     def x_copy(target, slot, c):
         return pltpu.make_async_remote_copy(
@@ -287,11 +386,10 @@
             device_id_type=MESH,
         )
 
+    pass_on(0)
     for c in range(chunks):
-        total = sbuf[s, c].astype(F32)
-        for d in range(1, senses):
-            z_copy(sens_peer(d), sens_peer(d), c).wait_recv()
-            total = total + rbuf[sens_peer(d), c].astype(F32)
+        pass_on(c + 1)
+        total = collect(c)
         high = total.astype(BF16)
         low = (total - high.astype(F32)).astype(BF16)
         stacked = jnp.concatenate([high, high, low], axis=0)
@@ -366,8 +464,7 @@
         for c in range(chunks):
             x_copy(freq_peer(d), f, c).wait_send()
     for c in range(chunks):
-        for d in range(1, senses):
-            z_copy(sens_peer(d), s, c).wait_send()
+        drain(c)
 
     @pl.when(has_left)
     def _():
@@ -415,6 +512,8 @@
             pltpu.VMEM((halves, block // senses, width), F32),
             pltpu.VMEM((senses, chunks, depth, width), BF16),
             pltpu.VMEM((senses, chunks, depth, width), BF16),
+            pltpu.VMEM((chunks, depth, width), BF16),
+            pltpu.VMEM((chunks, depth, width), BF16),
             pltpu.VMEM((chunks, rows, width), F32),
             pltpu.VMEM((groups, chunks, rows, width), BF16),
             pltpu.VMEM((groups, chunks, rows, width), BF16),
@@ -426,6 +525,8 @@
             dma((groups,)),
             dma((senses, chunks)),
             dma((senses, chunks)),
+            dma((chunks,)),
+            dma((chunks,)),
             dma((groups, chunks)),
             dma((groups, chunks)),
             dma((groups,)),

time: 31.7 us -> 29.7 us (0.937)
  Pallas kernels: 29.4 us -> 27.5 us
    pallas_call x1, Pallas kernels: 29.4 us -> 27.5 us  [local(): pl.pallas_call(functools.partial(body, (groups, params, senses, chunks)),...]
where the time goes in v2:
time: 29.7 us; the launch traced here: 29.2 us
  Pallas kernels  27.5 us (93%)
  local copies, waits for them, and re-layouts  1.74 us (6%)
    pallas_call x1, Pallas kernels, local(): pl.pallas_call(functools.partial(body, (groups, params, senses, chunks)),...  27.5 us
    reshape x1, local copies, waits for them, and re-layouts, local(): return out.reshape(time_dev, keep, cols)  1.74 us

profile of v2, /device:TPU:1, one launch (start us, length us, event | category | flops | bytes accessed | tf_op | source)
XLA Modules:
  0.0 29.2 jit_solution(16611527716215723464)
XLA Ops:
  0.0 27.5 %shard_map.73 = f32[52,1024]{1,0:T(8,128)} custom-call(bf16[208,150]{1,0:T(8,128)(2,1)} %bitcast.6, bf16[2,150,16,1024]{3,2,1,0:T(8,128)(2,1)} %bitcast.5, f32[16]{0:T(128)} %prior_hbm.1, f32[1,1024]{1,0:T(1,128)} %bitcast.7, bf16[2,2,32,416]{3,2,1,0:T(8,128)(2,1)} %constant.6.clone.spec_hbm, bf16[2,2,52,192]{3,2,1,0:T(8,128)(2,1)} %constant.7.clone.img_hbm, ...), custom_call_target="tpu_custom_call" | custom-call | tf_op jit(solution)/shard_map/pallas_call | solution.py:496
  27.5 1.7 %reshape.11 = f32[26,2,1024]{2,1,0:T(2,128)} reshape(f32[52,1024]{1,0:T(8,128)} %shard_map.73) | data formatting | bytes 425984 | tf_op jit(solution)/shard_map/reshape | solution.py:549
